TPU v7x, 32 devices: a whole 2x2x4 slice. The times are simulated.
32 devices in a mesh: row: 4 (over y, core), col: 8 (over z, x).
Axes of the slice: x: 2, y: 2, z: 4, core: 2. Of those that a mesh axis runs over, the one named last changes fastest.
Arguments:
- constraint: bfloat16 [8192, 16384], P('row', 'col'), may hold values from -0.046875 to 0.046875
- pattern: int32 [64, 128], P('row', 'col'), may hold values 0 or 1
- objective: float32 [16384, 256], P('col'), may hold values from -31 to 31
- row_bound: float32 [8192, 256], P('row'), may hold values from -31 to 31
- lower_bound: float32 [16384], P('col'), may hold values from -2 to -0.5
- upper_bound: float32 [16384], P('col'), may hold values from 0.5 to 2
Outputs:
- primal: float32 [16384, 256], P('col')
- dual_values: float32 [8192, 256], P('row')
- residual_norms: float32 [256], replicated
All inputs are finite; a program needn't handle non-finite values. No bound on the sum of `pattern` on one device may be relied on, other than what follows from the above.
Results may differ from a plain program's by a relative error of at most 0.0019.
Values may be sent and summed in bfloat16 or wider, within the bound.
No kernel may reach another device: no remote copies, remote signals or barrier semaphores. Data moves between devices by JAX's collectives and lax.ppermute only.
A program may use at most 128 MiB of HBM per device.

v0:
```python
import jax
import jax.numpy as jnp
from jax import lax
from jax.sharding import PartitionSpec as P

BLOCK = 128
ITERS = 3


step_primal = 0.6
step_dual = 0.6
epsilon = 1e-06


def masked(constraint, pattern):
    row_blocks, col_blocks = pattern.shape
    blocks = (
        constraint.reshape(row_blocks, BLOCK, col_blocks, BLOCK)
        * pattern.astype(jnp.bfloat16)[:, None, :, None]
    )
    return blocks.reshape(row_blocks * BLOCK, col_blocks * BLOCK)


def transposed(matrix, values):
    return lax.dot_general(
        matrix, values, (((0,), (0,)), ((), ())), preferred_element_type=jnp.float32
    )


def partial_stats(slack_share, displacement):
    return jnp.stack(
        [jnp.sum(jnp.maximum(slack_share, 0.0) ** 2, axis=0), jnp.sum(displacement**2, axis=0)]
    )


def settle(record):
    return lax.psum(record, ("row", "col"))


def on_device(constraint, pattern, objective, row_bound, lower_bound, upper_bound):
    matrix = masked(constraint, pattern)
    local_rows, local_cols = matrix.shape
    batch_size = objective.shape[1]
    row_devices = lax.axis_size("row")
    col_devices = lax.axis_size("col")
    total_rows = local_rows * row_devices
    total_cols = local_cols * col_devices
    row_share = local_rows // col_devices
    col_share = local_cols // row_devices
    row_offset = lax.axis_index("col") * row_share
    col_offset = lax.axis_index("row") * col_share
    records = []
    lower_share = lower_bound[:, None]
    upper_share = upper_bound[:, None]
    primal = jnp.zeros((local_cols, batch_size), jnp.float32)
    dual_values = jnp.zeros((local_rows, batch_size), jnp.float32)
    for iteration in range(ITERS):
        if iteration == 0:
            gradient = objective
        else:
            gradient = objective - lax.psum(
                transposed(matrix, dual_values.astype(jnp.bfloat16)), "row"
            )
        updated = jnp.clip(primal - step_primal * gradient, lower_share, upper_share)
        extrapolated = (2.0 * updated - primal).astype(jnp.bfloat16)
        product_rows = lax.psum(
            jnp.dot(matrix, extrapolated, preferred_element_type=jnp.float32), "col"
        )
        slack_rows = row_bound - product_rows
        dual_values = jnp.maximum(dual_values + step_dual * slack_rows, 0.0)
        slack_share = lax.dynamic_slice_in_dim(slack_rows, row_offset, row_share, 0)
        displacement = lax.dynamic_slice_in_dim(updated - primal, col_offset, col_share, 0)
        records.append(settle(partial_stats(slack_share, displacement)))
        primal = updated
    stacked = jnp.stack(records)
    residual_norms = jnp.zeros((batch_size,), jnp.float32)
    for iteration in range(ITERS):
        residual_norms = (
            residual_norms
            + jnp.sqrt(stacked[iteration, 0] / total_rows + epsilon)
            + jnp.sqrt(stacked[iteration, 1] / total_cols + epsilon)
        )
    return (primal, dual_values, residual_norms)


def solution(mesh):
    placed = (P("row", "col"), P("row", "col"), P("col", None), P("row", None), P("col"), P("col"))
    return jax.shard_map(
        on_device,
        mesh=mesh,
        in_specs=placed,
        out_specs=(P("col", None), P("row", None), P()),
        check_vma=False,
    )
```

profile of v0, /device:TPU:0, one launch (start us, length us, event | category | flops | bytes accessed | tf_op | source)
XLA Modules:
  0.0 529.3 jit_solution(18435655729704046118)
XLA Ops:
  7.2 0.7 convert_element_type.18
  7.9 1.1 mul.45
  9.1 2.2 copy-done.6
  11.3 1.9 bitcast_multiply_fusion
  13.2 3.2 copy-done.7
  16.4 3.9 fusion.3
  20.3 0.0 all-reduce.9.cloned.1.call-start
  20.4 105.1 %all-reduce.7.cloned.1.call-done = f32[2048,256]{1,0:T(8,128)} async-done(((f32[2048,256]{1,0:T(8,128)}), f32[2048,256]{1,0:T(8,128)}) %all-reduce.7.cloned.1.call-update) | async-done | bytes 2097168 | tf_op jit(solution)/shard_map/psum | solution.py:66
  125.5 1.9 sub.37
  127.4 1.4 copy-done.3
  128.8 7.2 %fusion.1 = f32[2048,256]{1,0:T(8,128)} fusion(bf16[2048,2048]{1,0:T(8,128)(2,1)} %copy-done.7, f32[2048,256]{1,0:T(8,128)S(1)} %sub.37), kind=kOutput, calls=%fused_computation.11 | convolution fusion | flops 2149056512 | bytes 12582912 | tf_op jit(solution)/shard_map/dot_general | solution.py:25
  136.1 50.8 %all-reduce.9.cloned.1.call-done = f32[2048,256]{1,0:T(8,128)} async-done(((f32[2048,256]{1,0:T(8,128)}), f32[2048,256]{1,0:T(8,128)}) %all-reduce.9.cloned.1.call-update) | async-done | bytes 2097168 | tf_op jit(solution)/shard_map/psum | solution.py:61
  186.9 2.7 maximum_minimum_fusion.1
  189.6 1.3 copy-done.1
  190.9 7.3 %fusion.4 = f32[2048,256]{1,0:T(8,128)} fusion(bf16[2048,2048]{1,0:T(8,128)(2,1)} %copy-done.7, f32[2048,256]{1,0:T(8,128)S(1)} %maximum_minimum_fusion.1, f32[2048,256]{1,0:T(8,128)S(1)} %copy-done.9, f32[2048]{0:T(1024)S(1)} %copy-done.11, f32[2048]{0:T(1024)S(1)} %copy-done.12), kind=kOutput, calls=%fused_computation.13 | convolution fusion | flops 2151153664 | bytes 14696448 | tf_op jit(solution)/shard_map/dot_general | solution.py:67
  198.2 0.2 all-reduce.13.cloned.1.call-start
  198.5 102.3 %all-reduce.11.cloned.1.call-done = f32[2048,256]{1,0:T(8,128)} async-done(((f32[2048,256]{1,0:T(8,128)}), f32[2048,256]{1,0:T(8,128)}) %all-reduce.11.cloned.1.call-update) | async-done | bytes 2097168 | tf_op jit(solution)/shard_map/psum | solution.py:66
  300.7 2.0 sub.41
  302.8 1.3 copy-done.5
  304.0 7.3 %fusion.6 = f32[2048,256]{1,0:T(8,128)} fusion(bf16[2048,2048]{1,0:T(8,128)(2,1)} %copy-done.7, f32[2048,256]{1,0:T(8,128)S(1)} %sub.41, f32[2048,256]{1,0:T(8,128)S(1)} %copy-done.4), kind=kOutput, calls=%fused_computation.15 | convolution fusion | flops 2150629376 | bytes 14680064 | tf_op jit(solution)/shard_map/dot_general | solution.py:25
  311.4 50.8 %all-reduce.13.cloned.1.call-done = f32[2048,256]{1,0:T(8,128)} async-done(((f32[2048,256]{1,0:T(8,128)}), f32[2048,256]{1,0:T(8,128)}) %all-reduce.13.cloned.1.call-update) | async-done | bytes 2097168 | tf_op jit(solution)/shard_map/psum | solution.py:61
  362.2 4.4 maximum_minimum_fusion.2
  366.6 1.3 copy-done.10
  367.9 7.1 %fusion.5 = f32[2048,256]{1,0:T(8,128)} fusion(bf16[2048,2048]{1,0:T(8,128)(2,1)} %copy-done.7, f32[2048,256]{1,0:T(8,128)S(1)} %copy-done.2, f32[2048,256]{1,0:T(8,128)S(1)} %get-tuple-element.12), kind=kOutput, calls=%fused_computation.14 | convolution fusion | flops 2149056512 | bytes 14680064 | tf_op jit(solution)/shard_map/dot_general | solution.py:67
  375.0 1.0 multiply_reduce_fusion.4
  376.0 1.0 multiply_reduce_fusion.3
  377.0 1.5 multiply_reduce_fusion.1
  378.5 99.0 %all-reduce.15.cloned.1.call-done = f32[2048,256]{1,0:T(8,128)} async-done(((f32[2048,256]{1,0:T(8,128)}), f32[2048,256]{1,0:T(8,128)}) %all-reduce.15.cloned.1.call-update) | async-done | bytes 2097168 | tf_op jit(solution)/shard_map/psum | solution.py:66
  477.5 4.9 add_maximum_fusion
  482.4 0.1 multiply_reduce_fusion.2
  482.4 39.8 %all-reduce = (f32[1,2,256]{2,1,0:T(2,128)S(1)}, f32[1,2,256]{2,1,0:T(2,128)S(1)}, f32[1,2,256]{2,1,0:T(2,128)S(1)}) all-reduce(f32[1,2,256]{2,1,0:T(2,128)S(1)} %maximum_bitcast_fusion.2, f32[1,2,256]{2,1,0:T(2,128)S(1)} %get-tuple-element.14, f32[1,2,256]{2,1,0:T(2,128)S(1)} %get-tuple-element.13), channel_id=1, replica_groups=mesh['row'=4,'col'=8] {'row','col'}, use_global_device_ids=true, to_apply=%region_13.14 | all-reduce | flops 1536 | bytes 12288 | tf_op jit(solution)/shard_map/psum | solution.py:37
  522.2 0.6 fusion.17
  (30 shorter events, 0.3 us)
Async XLA Ops:
  7.2 118.4 %all-reduce.7.cloned.1.call-start = ((), (), s32[]{:S(2)}) async-start(), calls=%async_computation | async-start | bytes 4194304 | tf_op jit(solution)/shard_map/psum | solution.py:66
  7.9 3.4 copy-start.6
  11.3 5.1 copy-start.8
  11.3 5.1 copy-start.11
  11.3 5.1 copy-start.12
  13.2 3.2 copy-start.7
  20.3 105.2 %copy-start = (f32[2048,256]{1,0:T(8,128)S(1)}, f32[2048,256]{1,0:T(8,128)}, u32[]{:S(2)}) copy-start(f32[2048,256]{1,0:T(8,128)} %param.9) | copy-start | bytes 6291460
  20.3 166.5 %all-reduce.9.cloned.1.call-start = ((), (), s32[]{:S(2)}) async-start(), calls=%async_computation.1 | async-start | bytes 4194304 | tf_op jit(solution)/shard_map/psum | solution.py:61
  127.4 1.4 copy-start.3
  136.0 164.7 %all-reduce.11.cloned.1.call-start = ((), (), s32[]{:S(2)}) async-start(), calls=%async_computation.2 | async-start | bytes 4194304 | tf_op jit(solution)/shard_map/psum | solution.py:66
  186.9 4.0 copy-start.9
  189.6 1.3 copy-start.1
  198.2 163.9 %all-reduce.13.cloned.1.call-start = ((), (), s32[]{:S(2)}) async-start(), calls=%async_computation.3 | async-start | bytes 4194304 | tf_op jit(solution)/shard_map/psum | solution.py:61
  300.7 3.3 copy-start.4
  302.7 1.3 copy-start.5
  311.3 166.1 %all-reduce.15.cloned.1.call-start = ((), (), s32[]{:S(2)}) async-start(), calls=%async_computation.4 | async-start | bytes 4194304 | tf_op jit(solution)/shard_map/psum | solution.py:66
  362.2 5.7 %copy-start.2 = (f32[2048,256]{1,0:T(8,128)S(1)}, f32[2048,256]{1,0:T(8,128)}, u32[]{:S(2)}) copy-start(f32[2048,256]{1,0:T(8,128)} %copy-done.1) | copy-start | bytes 6291460
  366.6 1.3 copy-start.10
Sparse Core Ops, SparseCore 0:
  20.5 105.0 all-reduce.6
  136.2 50.6 all-reduce.8
  198.3 102.3 all-reduce.10
  311.5 50.6 all-reduce.12
  375.1 102.3 all-reduce.14
where the time goes:
time: 530 us; the launch traced here: 529 us
  waiting for transfers between devices  408 us (77%)
  blocking collectives  39.8 us (8%)
  matrix products  32.8 us (6%)
  other arithmetic  22.6 us (4%)
  between operations  13.9 us (3%)
  local copies, waits for them, and re-layouts  11.9 us (2%)
    psum x3, waiting for transfers between devices, on_device(): lax.psum(jnp.dot(matrix, extrapolated, preferred_element_type=jnp.float32...  306 us
    psum x2, waiting for transfers between devices, on_device(): lax.psum(transposed(matrix, dual_values.astype(jnp.bfloat16)), 'row')  102 us
    psum x1, blocking collectives, settle(): return lax.psum(record, ('row', 'col'))  39.8 us
    dot_general x3, matrix products, on_device(): jnp.dot(matrix, extrapolated, preferred_element_type=jnp.float32)  18.3 us
    dot_general x2, matrix products, transposed(): lax.dot_general(matrix, values, (((0,), (0,)), ((), ())), preferred_eleme...  14.5 us
    unnamed x26, local copies, waits for them, and re-layouts  10.8 us
  transfers between devices with their start and end apart: 5, of which 5 were waited for; matrix products, arithmetic and copies ran while one was open for 1% of the time, Pallas kernels for 0%

commit v1 on v0

v1 whole, which is shorter than its diff:
```python
import jax
import jax.numpy as jnp
from jax import lax
from jax.experimental import pallas as pl
from jax.experimental.pallas import tpu as pltpu
from jax.sharding import PartitionSpec as P


BLOCK = 128
ITERS = 3
DIRECT_BITS = 2
MASK_ROWS = 256

step_primal = 0.6
step_dual = 0.6
epsilon = 1e-06

F32 = jnp.float32
BF16 = jnp.bfloat16


def bits_of(size):
    bits = size.bit_length() - 1
    assert size == 1 << bits
    return bits


def exchange(value, axis, distance):
    size = lax.axis_size(axis)
    return lax.ppermute(value, axis, [(i, i ^ distance) for i in range(size)])


def apart(*values):
    return lax.optimization_barrier(values)


def mask_kernel(half_ref, present_ref, block_ref, out_ref):
    rows = block_ref.shape[0]
    for r in range(rows // BLOCK):
        window = slice(r * BLOCK, (r + 1) * BLOCK)
        out_ref[window, :] = block_ref[window, :] * present_ref[0, r : r + 1, :]


def masked_half(constraint, present, half):
    local_rows, cols = constraint.shape
    rows = min(MASK_ROWS, local_rows // 2)
    steps = local_rows // 2 // rows
    source = lambda j, half: (half[0] * steps + j, 0)
    return pl.pallas_call(
        mask_kernel,
        grid_spec=pltpu.PrefetchScalarGridSpec(
            num_scalar_prefetch=1,
            grid=(steps,),
            in_specs=[
                pl.BlockSpec((1, rows // BLOCK, cols), lambda j, half: (half[0] * steps + j, 0, 0)),
                pl.BlockSpec((rows, cols), source),
            ],
            out_specs=pl.BlockSpec((rows, cols), lambda j, half: (j, 0)),
        ),
        out_shape=jax.ShapeDtypeStruct((local_rows // 2, cols), constraint.dtype),
        compiler_params=pltpu.CompilerParams(vmem_limit_bytes=8 << 20),
        name="mask",
    )(half.astype(jnp.int32)[None], present, constraint)


def presence(pattern, dtype):
    rows, cols = pattern.shape
    wide = jnp.broadcast_to(pattern.astype(dtype)[:, :, None], (rows, cols, BLOCK))
    return wide.reshape(rows * BLOCK // MASK_ROWS, MASK_ROWS // BLOCK, cols * BLOCK)


def in_place(pieces, block, bits):
    for d in range(bits):
        swap = ((block >> d) & 1) == 1
        pieces = [jnp.where(swap, pieces[t ^ (1 << d)], pieces[t]) for t in range(len(pieces))]
    return pieces


def spread_kernel(where_ref, *refs):
    (mine, other), out, sems = refs[:2], refs[-2], refs[-1]
    rows, lanes = mine.shape
    first = pl.multiple_of(where_ref[1], 8)
    copies = []
    for i, value in enumerate((mine, other)):
        left = pl.multiple_of((where_ref[0] ^ i) * lanes, lanes)
        copies.append(pltpu.make_async_copy(value, out.at[pl.ds(first, rows), pl.ds(left, lanes)], sems.at[i]))
    for copy in copies:
        copy.start()
    for copy in copies:
        copy.wait()


def spread(core, first, mine, other, shape, whole=None):
    anywhere = pl.BlockSpec(memory_space=pl.ANY)
    vmem = pl.BlockSpec(memory_space=pltpu.VMEM)
    where = jnp.stack([core, first]).astype(jnp.int32)
    inputs = [where, mine, other] + ([] if whole is None else [whole])
    return pl.pallas_call(
        spread_kernel,
        in_specs=[pl.BlockSpec(memory_space=pltpu.SMEM), vmem, vmem] + [anywhere] * (len(inputs) - 3),
        out_specs=anywhere,
        out_shape=jax.ShapeDtypeStruct(shape, F32),
        scratch_shapes=[pltpu.SemaphoreType.DMA((2,))],
        input_output_aliases={} if whole is None else {3: 0},
        compiler_params=pltpu.CompilerParams(vmem_limit_bytes=8 << 20),
        name="spread",
    )(*inputs)


def product(a, b):
    return jnp.dot(a, b, preferred_element_type=F32)


def transposed(a, b):
    return lax.dot_general(a, b, (((0,), (0,)), ((), ())), preferred_element_type=F32)


def iterations(constraint, pattern, objective, row_bound, lower_bound, upper_bound):
    local_rows, local_cols = constraint.shape
    batch = objective.shape[1]
    lanes = batch // 2
    row_devices = lax.axis_size("row")
    col_devices = lax.axis_size("col")
    row_bits = bits_of(row_devices)
    col_bits = bits_of(col_devices)
    total_rows = local_rows * row_devices
    total_cols = local_cols * col_devices
    half_rows = local_rows // 2
    share = local_rows // col_devices
    core = lax.axis_index("row") & 1
    col_index = lax.axis_index("col")
    bit = [(col_index >> b) & 1 for b in range(col_bits)]
    direct = range(max(1, col_bits - DIRECT_BITS), col_bits)
    halving = range(1, direct.start)
    peers = range(1, 1 << len(direct))
    block = sum(bit[b] << (col_bits - 1 - b) for b in direct)
    share_start = sum(bit[b] * (local_rows >> (b + 1)) for b in range(col_bits))
    halves = (bit[0] * half_rows, (1 - bit[0]) * half_rows)

    def distance(m):
        return sum(((m >> (col_bits - 1 - b)) & 1) << b for b in direct)

    lower = lower_bound[:, None]
    upper = upper_bound[:, None]

    def my_programs(value):
        return lax.dynamic_slice(value, (0, core * lanes), (value.shape[0], lanes))

    def their_programs(value):
        return lax.dynamic_slice(value, (0, (1 - core) * lanes), (value.shape[0], lanes))

    def first_step(cost):
        return (2.0 * jnp.clip(-step_primal * cost, lower, upper)).astype(BF16)

    send, received = [None] * 2, [None] * 2
    upper_rows, lower_rows = [None] * 2, [None] * 2
    own_presence = presence(pattern, constraint.dtype)
    upper_rows[0] = masked_half(constraint, own_presence, 1 - bit[0])
    wanted = my_programs(objective)
    (start,) = apart(first_step(wanted))
    (other_start,) = apart(first_step(their_programs(objective)))
    (send[0],) = apart(product(upper_rows[0], start).astype(BF16))
    received[0] = exchange(send[0], "col", 1)
    (theirs,) = apart(product(upper_rows[0], other_start).astype(BF16))
    send[1] = exchange(theirs, "row", 1)
    patterns = [pattern, exchange(pattern, "row", 1)]
    constraints = [constraint, exchange(constraint, "row", 1)]
    lower_rows[0] = masked_half(constraint, own_presence, bit[0])
    (theirs,) = apart(product(lower_rows[0], other_start))
    keep = [None, exchange(theirs, "row", 1)]
    (keep[0],) = apart(product(lower_rows[0], start))
    mine, theirs = apart(my_programs(row_bound), their_programs(row_bound))
    bound = [mine, exchange(theirs, "row", 1)]
    other_presence = presence(patterns[1], constraint.dtype)
    lower_rows[1] = masked_half(constraints[1], other_presence, bit[0])
    upper_rows[1] = masked_half(constraints[1], other_presence, 1 - bit[0])
    bound = list(apart(*bound))
    bound_half = [[lax.dynamic_slice_in_dim(bound[p], halves[h], half_rows, 0) for h in range(2)] for p in range(2)]
    bound_share = [lax.dynamic_slice_in_dim(bound[p], share_start, share, 0) for p in range(2)]
    wanted, *flat = apart(wanted, *bound_half[0], *bound_half[1], *bound_share)
    bound_half, bound_share = [flat[0:2], flat[2:4]], flat[4:]
    primal = None
    dual = [[None] * 2, [None] * 2]
    partial = None
    movement, violation = [], []
    joined = None

    def dual_step(old, slack):
        return jnp.maximum(step_dual * slack if old is None else old + step_dual * slack, 0.0)

    for iteration in range(ITERS):
        last = iteration + 1 == ITERS
        if iteration == 0:
            received[1] = exchange(send[1], "col", 1)
        else:
            for p in range(2):
                slack = bound_half[p][1] - received[p].astype(F32)
                dual[p][1] = dual_step(dual[p][1], slack)
                rounded = dual[p][1].astype(BF16)
                (more,) = apart(transposed(upper_rows[p], rounded))
                if p == 0:
                    (partial,) = apart(partial + more)
                else:
                    (partial,) = apart((partial + more).astype(BF16))
            own = partial
            for b in range(1, row_bits):
                arrived = exchange(own, "row", 1 << b)
                total = own.astype(F32) + arrived.astype(F32)
                if b + 1 < row_bits:
                    (own,) = apart(total.astype(BF16))
            if row_bits == 1:
                total = own.astype(F32)
            old = primal
            if old is None:
                old = jnp.clip(-step_primal * wanted, lower, upper)
            updated = jnp.clip(old - step_primal * (wanted - total), lower, upper)
            extrapolated = (2.0 * updated - old).astype(BF16)
            primal, old, extrapolated = apart(updated, old, extrapolated)
            for p in range(2):
                (send[p],) = apart(product(upper_rows[p], extrapolated).astype(BF16))
                received[p] = exchange(send[p], "col", 1)
            for p in range(2):
                (keep[p],) = apart(product(lower_rows[p], extrapolated))
            new, old, _ = apart(primal, old, keep[1])
            if iteration == 1:
                movement.append(jnp.sum(old**2, axis=0))
            movement.append(jnp.sum((new - old) ** 2, axis=0))
        total = jnp.stack([keep[p] + received[p].astype(F32) for p in range(2)])
        for b in halving:
            middle = total.shape[1] // 2
            away = lax.dynamic_slice_in_dim(total, (1 - bit[b]) * middle, middle, 1).astype(BF16)
            stay = lax.dynamic_slice_in_dim(total, bit[b] * middle, middle, 1)
            total = stay + exchange(away, "col", 1 << b).astype(F32)
        pieces = [
            jnp.stack(
                [
                    lax.dynamic_slice_in_dim(total[p], (block ^ m) * share, share, 0)
                    for p in range(2)
                ]
            )
            for m in range(1 + len(peers))
        ]
        stay, *pieces = apart(pieces[0], *(piece.astype(BF16) for piece in pieces[1:]))
        arrived = [exchange(piece, "col", distance(m)) for m, piece in zip(peers, pieces)]
        for piece in arrived:
            stay = stay + piece.astype(F32)
        slack = jnp.stack(bound_share) - stay
        violation.append(jnp.sum(jnp.maximum(slack, 0.0) ** 2, axis=(0, 1)))
        (mine,) = apart(stay.astype(BF16))
        pieces = [mine] + [exchange(mine, "col", distance(m)) for m in peers]
        pieces = in_place(pieces, block, len(direct))
        joined = list(apart(*(jnp.concatenate([piece[p] for piece in pieces], axis=0) for p in range(2))))
        for b in reversed(halving):
            both = jnp.stack(joined)
            other = exchange(both, "col", 1 << b)
            first = jnp.where(bit[b] == 0, both, other)
            second = jnp.where(bit[b] == 0, other, both)
            joined = list(jnp.concatenate([first, second], axis=1))
        for p in range(2):
            received[p] = exchange(joined[p], "col", 1)
        for p in range(2):
            slack = bound_half[p][0] - joined[p].astype(F32)
            dual[p][0] = dual_step(dual[p][0], slack)
            rounded = dual[p][0].astype(BF16)
            if not last:
                (more,) = apart(transposed(lower_rows[p], rounded))
                partial = more if p == 0 else partial + more

    (stats,) = apart(jnp.stack([*movement, *violation]))
    for b in [*halving, 0]:
        stats = stats + exchange(stats, "col", 1 << b)
    (stats,) = apart(stats)
    terms = [stats] + [exchange(stats, "col", distance(m)) for m in peers]
    while len(terms) > 1:
        terms = [terms[i] + terms[i + 1] for i in range(0, len(terms), 2)]
    (stats,) = terms
    moved, excess = stats[:ITERS], stats[ITERS:]
    for b in range(1, row_bits):
        excess = excess + exchange(excess, "row", 1 << b)
    norms = jnp.zeros((lanes,), F32)
    for iteration in range(ITERS):
        norms = (
            norms
            + jnp.sqrt(excess[iteration] / total_rows + epsilon)
            + jnp.sqrt(moved[iteration] / total_cols + epsilon)
        )
    other_norms = exchange(norms, "row", 1)
    other = exchange(primal, "row", 1)
    whole_primal = spread(core, 0, primal, other, (local_cols, batch))
    other = exchange(dual[1][0], "row", 1)
    whole_dual = spread(core, halves[0], dual[0][0], other, (local_rows, batch))
    whole_primal, whole_dual, *received = apart(whole_primal, whole_dual, *received)
    theirs = dual_step(dual[1][1], bound_half[1][1] - received[1].astype(F32))
    other = exchange(theirs, "row", 1)
    mine = dual_step(dual[0][1], bound_half[0][1] - received[0].astype(F32))
    whole_dual = spread(core, halves[1], mine, other, (local_rows, batch), whole_dual)
    residual_norms = jnp.where(core == 0, jnp.concatenate([norms, other_norms]), jnp.concatenate([other_norms, norms]))
    return (whole_primal, whole_dual, residual_norms)


def solution(mesh):
    placed = (P("row", "col"), P("row", "col"), P("col", None), P("row", None), P("col"), P("col"))
    return jax.shard_map(
        iterations,
        mesh=mesh,
        in_specs=placed,
        out_specs=(P("col", None), P("row", None), P()),
        check_vma=False,
    )
```

time: 530 us -> 224 us (0.42)
  waiting for transfers between devices: 408 us -> 102 us
  starting transfers between devices: 0.39 us -> 53.9 us
  blocking collectives: 39.8 us -> 0 us
  between operations: 13.9 us -> 1.84 us
  Pallas kernels: 0 us -> 11.8 us
  other arithmetic: 22.6 us -> 12.7 us
  matrix products: 32.8 us -> 27.1 us
    psum x5 -> x0, waiting for transfers between devices: 408 us -> none  [the longest x3 306 us: on_device(): lax.psum(jnp.dot(matrix, extrapolated, preferred_element_type=jnp.float32...]
    ppermute x0 -> x46, waiting for transfers between devices: none -> 102 us  [exchange(): return lax.ppermute(value, axis, [(i, i ^ distance) for i in range(size)])]
    ppermute x0 -> x46, starting transfers between devices: none -> 53.9 us  [exchange(): return lax.ppermute(value, axis, [(i, i ^ distance) for i in range(size)])]
    psum x1 -> x0, blocking collectives: 39.8 us -> none  [settle(): return lax.psum(record, ('row', 'col'))]
    pallas_call x0 -> x7, Pallas kernels: none -> 11.8 us  [the longest x4 6.81 us: masked_half(): pl.pallas_call(mask_kernel, grid_spec=pltpu.PrefetchScalarGridSpec(num_sc...]
    min x2 -> x0, other arithmetic: 7.11 us -> none  [on_device(): jnp.clip(primal - step_primal * gradient, lower_share, upper_share)]
    dot_general x5 -> x20, matrix products: 32.8 us -> 27.1 us  [the longest x12 16.5 us: product(): return jnp.dot(a, b, preferred_element_type=F32)]
    unnamed x26 -> x72, local copies, waits for them, and re-layouts: 10.8 us -> 9.68 us
  transfers between devices with their start and end apart: 5 -> 46, of which waited for: 5 -> 30; matrix products, arithmetic and copies ran while one was open for 1% -> 13% of each run, Pallas kernels for 0% -> 5%
where the time goes in v1:
time: 224 us
  waiting for transfers between devices  102 us (46%)
  starting transfers between devices  53.9 us (24%)
  matrix products  27.1 us (12%)
  local copies, waits for them, and re-layouts  14.5 us (6%)
  other arithmetic  12.7 us (6%)
  Pallas kernels  11.8 us (5%)
    ppermute x46, waiting for transfers between devices, exchange(): return lax.ppermute(value, axis, [(i, i ^ distance) for i in range(size)])  102 us
    ppermute x46, starting transfers between devices, exchange(): return lax.ppermute(value, axis, [(i, i ^ distance) for i in range(size)])  53.9 us
    dot_general x12, matrix products, product(): return jnp.dot(a, b, preferred_element_type=F32)  16.5 us
    dot_general x8, matrix products, transposed(): lax.dot_general(a, b, (((0,), (0,)), ((), ())), preferred_element_type=F32)  10.6 us
    unnamed x72, local copies, waits for them, and re-layouts  9.68 us
    pallas_call x4, Pallas kernels, masked_half(): pl.pallas_call(mask_kernel, grid_spec=pltpu.PrefetchScalarGridSpec(num_sc...  6.81 us
    pallas_call x3, Pallas kernels, spread(): pl.pallas_call(spread_kernel, in_specs=[pl.BlockSpec(memory_space=pltpu.S...  4.94 us
  transfers between devices with their start and end apart: 46, of which 30 were waited for; matrix products, arithmetic and copies ran while one was open for 13% of the time, Pallas kernels for 5%

profile of v1, /device:TPU:0, one launch (start us, length us, event | category | flops | bytes accessed | tf_op | source)
XLA Modules:
  0.0 223.9 jit_solution(4648217717392230850)
XLA Ops:
  4.0 3.4 %copy-done.5 = bf16[2048,2048]{1,0:T(8,128)(2,1)S(1)} copy-done((bf16[2048,2048]{1,0:T(8,128)(2,1)S(1)}, bf16[2048,2048]{1,0:T(8,128)(2,1)}, u32[]{:S(2)}) %copy-start.5) | copy-done | bytes 8388632
  11.2 3.4 %copy-done.6 = bf16[2048,2048]{1,0:T(8,128)(2,1)S(1)} copy-done((bf16[2048,2048]{1,0:T(8,128)(2,1)S(1)}, bf16[2048,2048]{1,0:T(8,128)(2,1)}, u32[]{:S(2)}) %copy-start.6) | copy-done | bytes 8388632
  19.5 2.5 %collective-permute-start.1 = (bf16[1024,128]{1,0:T(8,128)(2,1)}, bf16[1024,128]{1,0:T(8,128)(2,1)S(1)}, u32[]{:S(2)}, u32[]{:S(2)}) collective-permute-start(bf16[1024,128]{1,0:T(8,128)(2,1)} %convolution_convert_fusion.5), channel_id=1, source_target_pairs={{0,1},{1,0},{2,3},{3,2},{4,5},{5,4},{6,7},{7,6},{8,9},{9,8},{10,11... | collective-permute-start | bytes 786440 | tf_op jit(solution)/shard_map/ppermute | solution.py:30
  23.6 5.8 %collective-permute-done.1 = bf16[1024,128]{1,0:T(8,128)(2,1)S(1)} collective-permute-done((bf16[1024,128]{1,0:T(8,128)(2,1)}, bf16[1024,128]{1,0:T(8,128)(2,1)S(1)}, u32[]{:S(2)}, u32[]{:S(2)}) %collective-permute-start.1) | collective-permute-done | bytes 262176 | tf_op jit(solution)/shard_map/ppermute | solution.py:30
  29.5 5.3 %collective-permute-done.4 = bf16[1024,128]{1,0:T(8,128)(2,1)S(1)} collective-permute-done((bf16[1024,128]{1,0:T(8,128)(2,1)S(1)}, bf16[1024,128]{1,0:T(8,128)(2,1)S(1)}, u32[]{:S(2)}, u32[]{:S(2)}) %collective-permute-start.4) | collective-permute-done | bytes 262176 | tf_op jit(solution)/shard_map/ppermute | solution.py:30
  36.0 3.9 %collective-permute-start.7 = (bf16[2,256,128]{2,1,0:T(8,128)(2,1)S(1)}, bf16[2,256,128]{2,1,0:T(8,128)(2,1)S(1)}, u32[]{:S(2)}, u32[]{:S(2)}) collective-permute-start(bf16[2,256,128]{2,1,0:T(8,128)(2,1)S(1)} %pad_maximum_fusion.12), channel_id=1, source_target_pairs={{0,6},{1,7},{2,4},{3,5},{4,2},{5,3},{6,0},{7,1},{8,14},{9,15},{10,... | collective-permute-start | bytes 393224 | tf_op jit(solution)/shard_map/ppermute | solution.py:30
  40.6 3.7 %collective-permute-done.7 = bf16[2,256,128]{2,1,0:T(8,128)(2,1)S(1)} collective-permute-done((bf16[2,256,128]{2,1,0:T(8,128)(2,1)S(1)}, bf16[2,256,128]{2,1,0:T(8,128)(2,1)S(1)}, u32[]{:S(2)}, u32[]{:S(2)}) %collective-permute-start.7) | collective-permute-done | bytes 131104 | tf_op jit(solution)/shard_map/ppermute | solution.py:30
  44.3 2.7 %collective-permute-done.6 = bf16[2,256,128]{2,1,0:T(8,128)(2,1)S(1)} collective-permute-done((bf16[2,256,128]{2,1,0:T(8,128)(2,1)S(1)}, bf16[2,256,128]{2,1,0:T(8,128)(2,1)S(1)}, u32[]{:S(2)}, u32[]{:S(2)}) %collective-permute-start.6) | collective-permute-done | bytes 131104 | tf_op jit(solution)/shard_map/ppermute | solution.py:30
  47.0 3.8 %collective-permute-done.5 = bf16[2,256,128]{2,1,0:T(8,128)(2,1)S(1)} collective-permute-done((bf16[2,256,128]{2,1,0:T(8,128)(2,1)S(1)}, bf16[2,256,128]{2,1,0:T(8,128)(2,1)S(1)}, u32[]{:S(2)}, u32[]{:S(2)}) %collective-permute-start.5) | collective-permute-done | bytes 131104 | tf_op jit(solution)/shard_map/ppermute | solution.py:30
  50.9 2.5 %collective-permute-start.8 = (bf16[2,256,128]{2,1,0:T(8,128)(2,1)S(1)}, bf16[2,256,128]{2,1,0:T(8,128)(2,1)S(1)}, u32[]{:S(2)}, u32[]{:S(2)}) collective-permute-start(bf16[2,256,128]{2,1,0:T(8,128)(2,1)S(1)} %fusion.58), channel_id=1, source_target_pairs={{0,6},{1,7},{2,4},{3,5},{4,2},{5,3},{6,0},{7,1},{8,14},{9,15},{10,... | collective-permute-start | bytes 393224 | tf_op jit(solution)/shard_map/ppermute | solution.py:30
  56.7 2.4 %collective-permute-done.8 = bf16[2,256,128]{2,1,0:T(8,128)(2,1)S(1)} collective-permute-done((bf16[2,256,128]{2,1,0:T(8,128)(2,1)S(1)}, bf16[2,256,128]{2,1,0:T(8,128)(2,1)S(1)}, u32[]{:S(2)}, u32[]{:S(2)}) %collective-permute-start.8) | collective-permute-done | bytes 131104 | tf_op jit(solution)/shard_map/ppermute | solution.py:30
  59.1 3.5 %collective-permute-done.9 = bf16[2,256,128]{2,1,0:T(8,128)(2,1)S(1)} collective-permute-done((bf16[2,256,128]{2,1,0:T(8,128)(2,1)S(1)}, bf16[2,256,128]{2,1,0:T(8,128)(2,1)S(1)}, u32[]{:S(2)}, u32[]{:S(2)}) %collective-permute-start.9) | collective-permute-done | bytes 131104 | tf_op jit(solution)/shard_map/ppermute | solution.py:30
  68.0 4.8 %collective-permute-done.13 = bf16[1024,128]{1,0:T(8,128)(2,1)S(1)} collective-permute-done((bf16[1024,128]{1,0:T(8,128)(2,1)S(1)}, bf16[1024,128]{1,0:T(8,128)(2,1)S(1)}, u32[]{:S(2)}, u32[]{:S(2)}) %collective-permute-start.13) | collective-permute-done | bytes 262176 | tf_op jit(solution)/shard_map/ppermute | solution.py:30
  75.5 3.0 %mask.6 = bf16[1024,2048]{1,0:T(8,128)(2,1)S(1)} custom-call(s32[1]{0:T(128)} %bitcast.1.half_ref, bf16[8,2,2048]{2,1,0:T(2,128)(2,1)S(1)} %reshape.48.present_ref, bf16[2048,2048]{1,0:T(8,128)(2,1)} %collective-permute-done.12.block_ref), custom_call_target="tpu_custom_call" | custom-call | tf_op jit(solution)/shard_map/mask/pallas_call | solution.py:49
  80.0 3.0 %mask.7 = bf16[1024,2048]{1,0:T(8,128)(2,1)S(1)} custom-call(s32[1]{0:T(128)} %bitcast.2.half_ref, bf16[8,2,2048]{2,1,0:T(2,128)(2,1)S(1)} %reshape.48.present_ref, bf16[2048,2048]{1,0:T(8,128)(2,1)} %collective-permute-done.12.block_ref), custom_call_target="tpu_custom_call" | custom-call | tf_op jit(solution)/shard_map/mask/pallas_call | solution.py:49
  86.2 8.3 %collective-permute-done.15 = bf16[2048,128]{1,0:T(8,128)(2,1)S(1)} collective-permute-done((bf16[2048,128]{1,0:T(8,128)(2,1)S(1)}, bf16[2048,128]{1,0:T(8,128)(2,1)S(1)}, u32[]{:S(2)}, u32[]{:S(2)}) %collective-permute-start.15) | collective-permute-done | bytes 524320 | tf_op jit(solution)/shard_map/ppermute | solution.py:30
  102.5 3.0 %collective-permute-done.17 = bf16[1024,128]{1,0:T(8,128)(2,1)S(1)} collective-permute-done((bf16[1024,128]{1,0:T(8,128)(2,1)S(1)}, bf16[1024,128]{1,0:T(8,128)(2,1)S(1)}, u32[]{:S(2)}, u32[]{:S(2)}) %collective-permute-start.17) | collective-permute-done | bytes 262176 | tf_op jit(solution)/shard_map/ppermute | solution.py:30
  105.7 2.7 %collective-permute-done.16 = bf16[1024,128]{1,0:T(8,128)(2,1)S(1)} collective-permute-done((bf16[1024,128]{1,0:T(8,128)(2,1)S(1)}, bf16[1024,128]{1,0:T(8,128)(2,1)S(1)}, u32[]{:S(2)}, u32[]{:S(2)}) %collective-permute-start.16) | collective-permute-done | bytes 262176 | tf_op jit(solution)/shard_map/ppermute | solution.py:30
  108.6 5.9 %collective-permute-start.20 = (bf16[2,256,128]{2,1,0:T(8,128)(2,1)S(1)}, bf16[2,256,128]{2,1,0:T(8,128)(2,1)S(1)}, u32[]{:S(2)}, u32[]{:S(2)}) collective-permute-start(bf16[2,256,128]{2,1,0:T(8,128)(2,1)S(1)} %pad_maximum_fusion.15), channel_id=1, source_target_pairs={{0,6},{1,7},{2,4},{3,5},{4,2},{5,3},{6,0},{7,1},{8,14},{9,15},{10,... | collective-permute-start | bytes 393224 | tf_op jit(solution)/shard_map/ppermute | solution.py:30
  115.2 2.7 %collective-permute-done.20 = bf16[2,256,128]{2,1,0:T(8,128)(2,1)S(1)} collective-permute-done((bf16[2,256,128]{2,1,0:T(8,128)(2,1)S(1)}, bf16[2,256,128]{2,1,0:T(8,128)(2,1)S(1)}, u32[]{:S(2)}, u32[]{:S(2)}) %collective-permute-start.20) | collective-permute-done | bytes 131104 | tf_op jit(solution)/shard_map/ppermute | solution.py:30
  117.9 2.6 %collective-permute-done.19 = bf16[2,256,128]{2,1,0:T(8,128)(2,1)S(1)} collective-permute-done((bf16[2,256,128]{2,1,0:T(8,128)(2,1)S(1)}, bf16[2,256,128]{2,1,0:T(8,128)(2,1)S(1)}, u32[]{:S(2)}, u32[]{:S(2)}) %collective-permute-start.19) | collective-permute-done | bytes 131104 | tf_op jit(solution)/shard_map/ppermute | solution.py:30
  120.5 3.7 %collective-permute-done.18 = bf16[2,256,128]{2,1,0:T(8,128)(2,1)S(1)} collective-permute-done((bf16[2,256,128]{2,1,0:T(8,128)(2,1)S(1)}, bf16[2,256,128]{2,1,0:T(8,128)(2,1)S(1)}, u32[]{:S(2)}, u32[]{:S(2)}) %collective-permute-start.18) | collective-permute-done | bytes 131104 | tf_op jit(solution)/shard_map/ppermute | solution.py:30
  128.7 2.5 %collective-permute-done.21 = bf16[2,256,128]{2,1,0:T(8,128)(2,1)S(1)} collective-permute-done((bf16[2,256,128]{2,1,0:T(8,128)(2,1)S(1)}, bf16[2,256,128]{2,1,0:T(8,128)(2,1)S(1)}, u32[]{:S(2)}, u32[]{:S(2)}) %collective-permute-start.21) | collective-permute-done | bytes 131104 | tf_op jit(solution)/shard_map/ppermute | solution.py:30
  131.2 2.7 %collective-permute-done.22 = bf16[2,256,128]{2,1,0:T(8,128)(2,1)S(1)} collective-permute-done((bf16[2,256,128]{2,1,0:T(8,128)(2,1)S(1)}, bf16[2,256,128]{2,1,0:T(8,128)(2,1)S(1)}, u32[]{:S(2)}, u32[]{:S(2)}) %collective-permute-start.22) | collective-permute-done | bytes 131104 | tf_op jit(solution)/shard_map/ppermute | solution.py:30
  147.5 6.7 %collective-permute-done.26 = bf16[2048,128]{1,0:T(8,128)(2,1)S(1)} collective-permute-done((bf16[2048,128]{1,0:T(8,128)(2,1)S(1)}, bf16[2048,128]{1,0:T(8,128)(2,1)S(1)}, u32[]{:S(2)}, u32[]{:S(2)}) %collective-permute-start.26) | collective-permute-done | bytes 524320 | tf_op jit(solution)/shard_map/ppermute | solution.py:30
  162.3 3.0 %collective-permute-done.29 = bf16[1024,128]{1,0:T(8,128)(2,1)S(1)} collective-permute-done((bf16[1024,128]{1,0:T(8,128)(2,1)S(1)}, bf16[1024,128]{1,0:T(8,128)(2,1)S(1)}, u32[]{:S(2)}, u32[]{:S(2)}) %collective-permute-start.29) | collective-permute-done | bytes 262176 | tf_op jit(solution)/shard_map/ppermute | solution.py:30
  165.4 2.7 %collective-permute-done.28 = bf16[1024,128]{1,0:T(8,128)(2,1)S(1)} collective-permute-done((bf16[1024,128]{1,0:T(8,128)(2,1)S(1)}, bf16[1024,128]{1,0:T(8,128)(2,1)S(1)}, u32[]{:S(2)}, u32[]{:S(2)}) %collective-permute-start.28) | collective-permute-done | bytes 262176 | tf_op jit(solution)/shard_map/ppermute | solution.py:30
  170.5 2.4 %collective-permute-start.30 = (bf16[2,256,128]{2,1,0:T(8,128)(2,1)S(1)}, bf16[2,256,128]{2,1,0:T(8,128)(2,1)S(1)}, u32[]{:S(2)}, u32[]{:S(2)}) collective-permute-start(bf16[2,256,128]{2,1,0:T(8,128)(2,1)S(1)} %pad_maximum_fusion.16), channel_id=1, source_target_pairs={{0,4},{1,5},{2,6},{3,7},{4,0},{5,1},{6,2},{7,3},{8,12},{9,13},{10,... | collective-permute-start | bytes 393224 | tf_op jit(solution)/shard_map/ppermute | solution.py:30
  175.3 2.8 %collective-permute-done.31 = bf16[2,256,128]{2,1,0:T(8,128)(2,1)S(1)} collective-permute-done((bf16[2,256,128]{2,1,0:T(8,128)(2,1)S(1)}, bf16[2,256,128]{2,1,0:T(8,128)(2,1)S(1)}, u32[]{:S(2)}, u32[]{:S(2)}) %collective-permute-start.31) | collective-permute-done | bytes 131104 | tf_op jit(solution)/shard_map/ppermute | solution.py:30
  195.0 3.3 %collective-permute-done.34 = bf16[2,256,128]{2,1,0:T(8,128)(2,1)S(1)} collective-permute-done((bf16[2,256,128]{2,1,0:T(8,128)(2,1)S(1)}, bf16[2,256,128]{2,1,0:T(8,128)(2,1)S(1)}, u32[]{:S(2)}, u32[]{:S(2)}) %collective-permute-start.34) | collective-permute-done | bytes 131104 | tf_op jit(solution)/shard_map/ppermute | solution.py:30
  198.3 3.8 %collective-permute-done.35 = bf16[2,256,128]{2,1,0:T(8,128)(2,1)S(1)} collective-permute-done((bf16[2,256,128]{2,1,0:T(8,128)(2,1)S(1)}, bf16[2,256,128]{2,1,0:T(8,128)(2,1)S(1)}, u32[]{:S(2)}, u32[]{:S(2)}) %collective-permute-start.35) | collective-permute-done | bytes 131104 | tf_op jit(solution)/shard_map/ppermute | solution.py:30
  209.6 8.6 %collective-permute-done.37 = bf16[1024,128]{1,0:T(8,128)(2,1)S(1)} collective-permute-done((bf16[1024,128]{1,0:T(8,128)(2,1)S(1)}, bf16[1024,128]{1,0:T(8,128)(2,1)S(1)}, u32[]{:S(2)}, u32[]{:S(2)}) %collective-permute-start.37) | collective-permute-done | bytes 262176 | tf_op jit(solution)/shard_map/ppermute | solution.py:30
  (243 shorter events, 100.9 us)
Async XLA Ops:
  0.6 74.9 %collective-permute-start.12 = (bf16[2048,2048]{1,0:T(8,128)(2,1)}, bf16[2048,2048]{1,0:T(8,128)(2,1)}, u32[]{:S(2)}, u32[]{:S(2)}) collective-permute-start(bf16[2048,2048]{1,0:T(8,128)(2,1)} %block_ref.3), channel_id=1, source_target_pairs={{0,8},{8,0},{16,24},{24,16},{1,9},{9,1},{17,25},{25,17},{2,10},{10... | collective-permute-start | bytes 25165832 | tf_op jit(solution)/shard_map/ppermute | solution.py:30
  11.1 18.4 %collective-permute-start.2 = (f32[1024,128]{1,0:T(8,128)S(1)}, f32[1024,128]{1,0:T(8,128)}, u32[]{:S(2)}, u32[]{:S(2)}) collective-permute-start(f32[1024,128]{1,0:T(8,128)S(1)} %fusion.78), channel_id=1, source_target_pairs={{0,8},{8,0},{16,24},{24,16},{1,9},{9,1},{17,25},{25,17},{2,10},{10... | collective-permute-start | bytes 1572872 | tf_op jit(solution)/shard_map/ppermute | solution.py:30
  19.5 9.9 %collective-permute-start.1 = (bf16[1024,128]{1,0:T(8,128)(2,1)}, bf16[1024,128]{1,0:T(8,128)(2,1)S(1)}, u32[]{:S(2)}, u32[]{:S(2)}) collective-permute-start(bf16[1024,128]{1,0:T(8,128)(2,1)} %convolution_convert_fusion.5), channel_id=1, source_target_pairs={{0,1},{1,0},{2,3},{3,2},{4,5},{5,4},{6,7},{7,6},{8,9},{9,8},{10,11... | collective-permute-start | bytes 786440 | tf_op jit(solution)/shard_map/ppermute | solution.py:30
  23.3 11.5 %collective-permute-start.4 = (bf16[1024,128]{1,0:T(8,128)(2,1)S(1)}, bf16[1024,128]{1,0:T(8,128)(2,1)S(1)}, u32[]{:S(2)}, u32[]{:S(2)}) collective-permute-start(bf16[1024,128]{1,0:T(8,128)(2,1)S(1)} %collective-permute-done.3), channel_id=1, source_target_pairs={{0,1},{1,0},{2,3},{3,2},{4,5},{5,4},{6,7},{7,6},{8,9},{9,8},{10,11... | collective-permute-start | bytes 786440 | tf_op jit(solution)/shard_map/ppermute | solution.py:30
  36.0 8.3 %collective-permute-start.7 = (bf16[2,256,128]{2,1,0:T(8,128)(2,1)S(1)}, bf16[2,256,128]{2,1,0:T(8,128)(2,1)S(1)}, u32[]{:S(2)}, u32[]{:S(2)}) collective-permute-start(bf16[2,256,128]{2,1,0:T(8,128)(2,1)S(1)} %pad_maximum_fusion.12), channel_id=1, source_target_pairs={{0,6},{1,7},{2,4},{3,5},{4,2},{5,3},{6,0},{7,1},{8,14},{9,15},{10,... | collective-permute-start | bytes 393224 | tf_op jit(solution)/shard_map/ppermute | solution.py:30
  39.9 7.1 %collective-permute-start.6 = (bf16[2,256,128]{2,1,0:T(8,128)(2,1)S(1)}, bf16[2,256,128]{2,1,0:T(8,128)(2,1)S(1)}, u32[]{:S(2)}, u32[]{:S(2)}) collective-permute-start(bf16[2,256,128]{2,1,0:T(8,128)(2,1)S(1)} %get-tuple-element.54), channel_id=1, source_target_pairs={{0,2},{1,3},{2,0},{3,1},{4,6},{5,7},{6,4},{7,5},{8,10},{9,11},{10,... | collective-permute-start | bytes 393224 | tf_op jit(solution)/shard_map/ppermute | solution.py:30
  39.9 10.9 %collective-permute-start.5 = (bf16[2,256,128]{2,1,0:T(8,128)(2,1)S(1)}, bf16[2,256,128]{2,1,0:T(8,128)(2,1)S(1)}, u32[]{:S(2)}, u32[]{:S(2)}) collective-permute-start(bf16[2,256,128]{2,1,0:T(8,128)(2,1)S(1)} %get-tuple-element.53), channel_id=1, source_target_pairs={{0,4},{1,5},{2,6},{3,7},{4,0},{5,1},{6,2},{7,3},{8,12},{9,13},{10,... | collective-permute-start | bytes 393224 | tf_op jit(solution)/shard_map/ppermute | solution.py:30
  40.6 15.9 %collective-permute-start.11 = (s32[16,16]{1,0:T(8,128)S(1)}, s32[16,16]{1,0:T(8,128)S(1)}, u32[]{:S(2)}, u32[]{:S(2)}) collective-permute-start(s32[16,16]{1,0:T(8,128)S(1)} %copy-done.35), channel_id=1, source_target_pairs={{0,8},{8,0},{16,24},{24,16},{1,9},{9,1},{17,25},{25,17},{2,10},{10... | collective-permute-start | bytes 3080 | tf_op jit(solution)/shard_map/ppermute | solution.py:30
  50.9 8.2 %collective-permute-start.8 = (bf16[2,256,128]{2,1,0:T(8,128)(2,1)S(1)}, bf16[2,256,128]{2,1,0:T(8,128)(2,1)S(1)}, u32[]{:S(2)}, u32[]{:S(2)}) collective-permute-start(bf16[2,256,128]{2,1,0:T(8,128)(2,1)S(1)} %fusion.58), channel_id=1, source_target_pairs={{0,6},{1,7},{2,4},{3,5},{4,2},{5,3},{6,0},{7,1},{8,14},{9,15},{10,... | collective-permute-start | bytes 393224 | tf_op jit(solution)/shard_map/ppermute | solution.py:30
  53.4 9.1 %collective-permute-start.9 = (bf16[2,256,128]{2,1,0:T(8,128)(2,1)S(1)}, bf16[2,256,128]{2,1,0:T(8,128)(2,1)S(1)}, u32[]{:S(2)}, u32[]{:S(2)}) collective-permute-start(bf16[2,256,128]{2,1,0:T(8,128)(2,1)S(1)} %fusion.58), channel_id=1, source_target_pairs={{0,2},{1,3},{2,0},{3,1},{4,6},{5,7},{6,4},{7,5},{8,10},{9,11},{10,... | collective-permute-start | bytes 393224 | tf_op jit(solution)/shard_map/ppermute | solution.py:30
  53.4 10.0 %collective-permute-start.10 = (bf16[2,256,128]{2,1,0:T(8,128)(2,1)S(1)}, bf16[2,256,128]{2,1,0:T(8,128)(2,1)S(1)}, u32[]{:S(2)}, u32[]{:S(2)}) collective-permute-start(bf16[2,256,128]{2,1,0:T(8,128)(2,1)S(1)} %fusion.58), channel_id=1, source_target_pairs={{0,4},{1,5},{2,6},{3,7},{4,0},{5,1},{6,2},{7,3},{8,12},{9,13},{10,... | collective-permute-start | bytes 393224 | tf_op jit(solution)/shard_map/ppermute | solution.py:30
  56.5 9.2 %collective-permute-start = (f32[2048,128]{1,0:T(8,128)}, f32[2048,128]{1,0:T(8,128)}, u32[]{:S(2)}, u32[]{:S(2)}) collective-permute-start(f32[2048,128]{1,0:T(8,128)} %get-tuple-element.47), channel_id=1, source_target_pairs={{0,8},{8,0},{16,24},{24,16},{1,9},{9,1},{17,25},{25,17},{2,10},{10... | collective-permute-start | bytes 3145736 | tf_op jit(solution)/shard_map/ppermute | solution.py:30
  63.6 9.2 %collective-permute-start.13 = (bf16[1024,128]{1,0:T(8,128)(2,1)S(1)}, bf16[1024,128]{1,0:T(8,128)(2,1)S(1)}, u32[]{:S(2)}, u32[]{:S(2)}) collective-permute-start(bf16[1024,128]{1,0:T(8,128)(2,1)S(1)} %pad_maximum_fusion.1), channel_id=1, source_target_pairs={{0,1},{1,0},{2,3},{3,2},{4,5},{5,4},{6,7},{7,6},{8,9},{9,8},{10,11... | collective-permute-start | bytes 786440 | tf_op jit(solution)/shard_map/ppermute | solution.py:30
  65.2 17.9 %collective-permute-start.14 = (bf16[1024,128]{1,0:T(8,128)(2,1)S(1)}, bf16[1024,128]{1,0:T(8,128)(2,1)S(1)}, u32[]{:S(2)}, u32[]{:S(2)}) collective-permute-start(bf16[1024,128]{1,0:T(8,128)(2,1)S(1)} %pad_maximum_fusion.2), channel_id=1, source_target_pairs={{0,1},{1,0},{2,3},{3,2},{4,5},{5,4},{6,7},{7,6},{8,9},{9,8},{10,11... | collective-permute-start | bytes 786440 | tf_op jit(solution)/shard_map/ppermute | solution.py:30
  84.6 9.9 %collective-permute-start.15 = (bf16[2048,128]{1,0:T(8,128)(2,1)S(1)}, bf16[2048,128]{1,0:T(8,128)(2,1)S(1)}, u32[]{:S(2)}, u32[]{:S(2)}) collective-permute-start(bf16[2048,128]{1,0:T(8,128)(2,1)S(1)} %add_convert_fusion.1), channel_id=1, source_target_pairs={{0,16},{8,24},{16,0},{24,8},{1,17},{9,25},{17,1},{25,9},{2,18},{10... | collective-permute-start | bytes 1572872 | tf_op jit(solution)/shard_map/ppermute | solution.py:30
  108.6 9.3 %collective-permute-start.20 = (bf16[2,256,128]{2,1,0:T(8,128)(2,1)S(1)}, bf16[2,256,128]{2,1,0:T(8,128)(2,1)S(1)}, u32[]{:S(2)}, u32[]{:S(2)}) collective-permute-start(bf16[2,256,128]{2,1,0:T(8,128)(2,1)S(1)} %pad_maximum_fusion.15), channel_id=1, source_target_pairs={{0,6},{1,7},{2,4},{3,5},{4,2},{5,3},{6,0},{7,1},{8,14},{9,15},{10,... | collective-permute-start | bytes 393224 | tf_op jit(solution)/shard_map/ppermute | solution.py:30
  114.5 9.7 %collective-permute-start.18 = (bf16[2,256,128]{2,1,0:T(8,128)(2,1)S(1)}, bf16[2,256,128]{2,1,0:T(8,128)(2,1)S(1)}, u32[]{:S(2)}, u32[]{:S(2)}) collective-permute-start(bf16[2,256,128]{2,1,0:T(8,128)(2,1)S(1)} %pad_maximum_fusion.13), channel_id=1, source_target_pairs={{0,4},{1,5},{2,6},{3,7},{4,0},{5,1},{6,2},{7,3},{8,12},{9,13},{10,... | collective-permute-start | bytes 393224 | tf_op jit(solution)/shard_map/ppermute | solution.py:30
  124.3 6.9 %collective-permute-start.21 = (bf16[2,256,128]{2,1,0:T(8,128)(2,1)S(1)}, bf16[2,256,128]{2,1,0:T(8,128)(2,1)S(1)}, u32[]{:S(2)}, u32[]{:S(2)}) collective-permute-start(bf16[2,256,128]{2,1,0:T(8,128)(2,1)S(1)} %fusion.59), channel_id=1, source_target_pairs={{0,6},{1,7},{2,4},{3,5},{4,2},{5,3},{6,0},{7,1},{8,14},{9,15},{10,... | collective-permute-start | bytes 393224 | tf_op jit(solution)/shard_map/ppermute | solution.py:30
  126.5 7.4 %collective-permute-start.22 = (bf16[2,256,128]{2,1,0:T(8,128)(2,1)S(1)}, bf16[2,256,128]{2,1,0:T(8,128)(2,1)S(1)}, u32[]{:S(2)}, u32[]{:S(2)}) collective-permute-start(bf16[2,256,128]{2,1,0:T(8,128)(2,1)S(1)} %fusion.59), channel_id=1, source_target_pairs={{0,2},{1,3},{2,0},{3,1},{4,6},{5,7},{6,4},{7,5},{8,10},{9,11},{10,... | collective-permute-start | bytes 393224 | tf_op jit(solution)/shard_map/ppermute | solution.py:30
  126.5 7.4 %collective-permute-start.23 = (bf16[2,256,128]{2,1,0:T(8,128)(2,1)S(1)}, bf16[2,256,128]{2,1,0:T(8,128)(2,1)S(1)}, u32[]{:S(2)}, u32[]{:S(2)}) collective-permute-start(bf16[2,256,128]{2,1,0:T(8,128)(2,1)S(1)} %fusion.59), channel_id=1, source_target_pairs={{0,4},{1,5},{2,6},{3,7},{4,0},{5,1},{6,2},{7,3},{8,12},{9,13},{10,... | collective-permute-start | bytes 393224 | tf_op jit(solution)/shard_map/ppermute | solution.py:30
  144.9 9.2 %collective-permute-start.26 = (bf16[2048,128]{1,0:T(8,128)(2,1)S(1)}, bf16[2048,128]{1,0:T(8,128)(2,1)S(1)}, u32[]{:S(2)}, u32[]{:S(2)}) collective-permute-start(bf16[2048,128]{1,0:T(8,128)(2,1)S(1)} %add_convert_fusion), channel_id=1, source_target_pairs={{0,16},{8,24},{16,0},{24,8},{1,17},{9,25},{17,1},{25,9},{2,18},{10... | collective-permute-start | bytes 1572872 | tf_op jit(solution)/shard_map/ppermute | solution.py:30
  161.6 6.5 %collective-permute-start.28 = (bf16[1024,128]{1,0:T(8,128)(2,1)S(1)}, bf16[1024,128]{1,0:T(8,128)(2,1)S(1)}, u32[]{:S(2)}, u32[]{:S(2)}) collective-permute-start(bf16[1024,128]{1,0:T(8,128)(2,1)S(1)} %convolution_convert_fusion.1), channel_id=1, source_target_pairs={{0,1},{1,0},{2,3},{3,2},{4,5},{5,4},{6,7},{7,6},{8,9},{9,8},{10,11... | collective-permute-start | bytes 786440 | tf_op jit(solution)/shard_map/ppermute | solution.py:30
  168.4 7.0 %collective-permute-start.32 = (bf16[2,256,128]{2,1,0:T(8,128)(2,1)S(1)}, bf16[2,256,128]{2,1,0:T(8,128)(2,1)S(1)}, u32[]{:S(2)}, u32[]{:S(2)}) collective-permute-start(bf16[2,256,128]{2,1,0:T(8,128)(2,1)S(1)} %pad_maximum_fusion.18), channel_id=1, source_target_pairs={{0,6},{1,7},{2,4},{3,5},{4,2},{5,3},{6,0},{7,1},{8,14},{9,15},{10,... | collective-permute-start | bytes 393224 | tf_op jit(solution)/shard_map/ppermute | solution.py:30
  170.5 7.6 %collective-permute-start.31 = (bf16[2,256,128]{2,1,0:T(8,128)(2,1)S(1)}, bf16[2,256,128]{2,1,0:T(8,128)(2,1)S(1)}, u32[]{:S(2)}, u32[]{:S(2)}) collective-permute-start(bf16[2,256,128]{2,1,0:T(8,128)(2,1)S(1)} %pad_maximum_fusion.17), channel_id=1, source_target_pairs={{0,2},{1,3},{2,0},{3,1},{4,6},{5,7},{6,4},{7,5},{8,10},{9,11},{10,... | collective-permute-start | bytes 393224 | tf_op jit(solution)/shard_map/ppermute | solution.py:30
  170.5 7.6 %collective-permute-start.30 = (bf16[2,256,128]{2,1,0:T(8,128)(2,1)S(1)}, bf16[2,256,128]{2,1,0:T(8,128)(2,1)S(1)}, u32[]{:S(2)}, u32[]{:S(2)}) collective-permute-start(bf16[2,256,128]{2,1,0:T(8,128)(2,1)S(1)} %pad_maximum_fusion.16), channel_id=1, source_target_pairs={{0,4},{1,5},{2,6},{3,7},{4,0},{5,1},{6,2},{7,3},{8,12},{9,13},{10,... | collective-permute-start | bytes 393224 | tf_op jit(solution)/shard_map/ppermute | solution.py:30
  186.8 19.3 %collective-permute-start.27 = (f32[2048,128]{1,0:T(8,128)S(1)}, f32[2048,128]{1,0:T(8,128)S(1)}, u32[]{:S(2)}, u32[]{:S(2)}) collective-permute-start(f32[2048,128]{1,0:T(8,128)S(1)} %get-tuple-element.85.refs_0_), channel_id=1, source_target_pairs={{0,8},{8,0},{16,24},{24,16},{1,9},{9,1},{17,25},{25,17},{2,10},{10... | collective-permute-start | bytes 3145736 | tf_op jit(solution)/shard_map/ppermute | solution.py:30
  186.8 8.2 %collective-permute-start.33 = (bf16[2,256,128]{2,1,0:T(8,128)(2,1)S(1)}, bf16[2,256,128]{2,1,0:T(8,128)(2,1)S(1)}, u32[]{:S(2)}, u32[]{:S(2)}) collective-permute-start(bf16[2,256,128]{2,1,0:T(8,128)(2,1)S(1)} %get-tuple-element.108), channel_id=1, source_target_pairs={{0,6},{1,7},{2,4},{3,5},{4,2},{5,3},{6,0},{7,1},{8,14},{9,15},{10,... | collective-permute-start | bytes 393224 | tf_op jit(solution)/shard_map/ppermute | solution.py:30
  188.9 9.4 %collective-permute-start.34 = (bf16[2,256,128]{2,1,0:T(8,128)(2,1)S(1)}, bf16[2,256,128]{2,1,0:T(8,128)(2,1)S(1)}, u32[]{:S(2)}, u32[]{:S(2)}) collective-permute-start(bf16[2,256,128]{2,1,0:T(8,128)(2,1)S(1)} %get-tuple-element.108), channel_id=1, source_target_pairs={{0,2},{1,3},{2,0},{3,1},{4,6},{5,7},{6,4},{7,5},{8,10},{9,11},{10,... | collective-permute-start | bytes 393224 | tf_op jit(solution)/shard_map/ppermute | solution.py:30
  189.5 12.6 %collective-permute-start.35 = (bf16[2,256,128]{2,1,0:T(8,128)(2,1)S(1)}, bf16[2,256,128]{2,1,0:T(8,128)(2,1)S(1)}, u32[]{:S(2)}, u32[]{:S(2)}) collective-permute-start(bf16[2,256,128]{2,1,0:T(8,128)(2,1)S(1)} %get-tuple-element.108), channel_id=1, source_target_pairs={{0,4},{1,5},{2,6},{3,7},{4,0},{5,1},{6,2},{7,3},{8,12},{9,13},{10,... | collective-permute-start | bytes 393224 | tf_op jit(solution)/shard_map/ppermute | solution.py:30
  191.2 12.5 %collective-permute-start.44 = (f32[3,128]{1,0:T(4,128)S(1)}, f32[3,128]{1,0:T(4,128)S(1)}, u32[]{:S(2)}, u32[]{:S(2)}) collective-permute-start(f32[3,128]{1,0:T(4,128)S(1)} %slice.121), channel_id=1, source_target_pairs={{0,16},{8,24},{16,0},{24,8},{1,17},{9,25},{17,1},{25,9},{2,18},{10... | collective-permute-start | bytes 4616 | tf_op jit(solution)/shard_map/ppermute | solution.py:30
  203.7 14.4 %collective-permute-start.38 = (bf16[1024,128]{1,0:T(8,128)(2,1)S(1)}, bf16[1024,128]{1,0:T(8,128)(2,1)S(1)}, u32[]{:S(2)}, u32[]{:S(2)}) collective-permute-start(bf16[1024,128]{1,0:T(8,128)(2,1)S(1)} %pad_maximum_fusion.8), channel_id=1, source_target_pairs={{0,1},{1,0},{2,3},{3,2},{4,5},{5,4},{6,7},{7,6},{8,9},{9,8},{10,11... | collective-permute-start | bytes 786440 | tf_op jit(solution)/shard_map/ppermute | solution.py:30
  205.2 12.9 %collective-permute-start.37 = (bf16[1024,128]{1,0:T(8,128)(2,1)S(1)}, bf16[1024,128]{1,0:T(8,128)(2,1)S(1)}, u32[]{:S(2)}, u32[]{:S(2)}) collective-permute-start(bf16[1024,128]{1,0:T(8,128)(2,1)S(1)} %pad_maximum_fusion.7), channel_id=1, source_target_pairs={{0,1},{1,0},{2,3},{3,2},{4,5},{5,4},{6,7},{7,6},{8,9},{9,8},{10,11... | collective-permute-start | bytes 786440 | tf_op jit(solution)/shard_map/ppermute | solution.py:30
  (50 other events, 792.8 us)
